TPU v7x, 32 devices: a whole 2x2x4 slice. The times are simulated.
32 devices in a mesh: lag: 2 (over core), space: 16 (over z, y, x).
Axes of the slice: x: 2, y: 2, z: 4, core: 2. Of those that a mesh axis runs over, the one named last changes fastest.
Arguments:
- ensemble: bfloat16 [2, 64, 65536], P('lag', None, 'space'), may hold values from -6 to 6
- obs_pert: bfloat16 [2, 64, 16384], P('lag', None, 'space'), may hold values from -6 to 6
- obs_innov: bfloat16 [2, 16384], P('lag', 'space'), may hold values from -12 to 12
- obs_rinv: bfloat16 [2, 16384], P('lag', 'space'), may hold values from 0.019897461 to 0.5
- obs_tile: int32 [2, 16384, 1], P('lag', 'space'), may hold values from 0 to 15; in each aligned block of 1024 rows (0 to 1023, 1024 to 2047, ..., all dimensions but the last counted through in order) at most 128 rows name the same one
- obs_column: int32 [2, 16384], P('lag', 'space'), may hold values from 0 to 4095
- obs_count: int32 [2, 16], P('lag', 'space'), may hold values from 512 to 1024, as said below
Outputs:
- analysis: bfloat16 [2, 64, 65536], P('lag', None, 'space')
Inputs may be any that keep to these rules, and one draw needn't show every extreme that they name: `obs_tile`: among the 1024 slots of one device at one lag, no tile is named more than 128 times. `obs_count`: slots of a device past its count are not used; in every draw some device uses all 1024.
All inputs are finite; a program needn't handle non-finite values.
Results may differ from a plain program's by a relative error of at most 0.0022.
The roundings to bfloat16 on the way count: a program that leaves them out, or rounds other values in their place, can miss the bound.
Values may be sent and summed in bfloat16 or wider, within the bound.
A program may use at most 64 MiB of HBM per device.

v0:
```python
import math

import jax
import jax.numpy as jnp
from jax import lax
from jax.sharding import PartitionSpec as P

SPACING = 512
NS_ITERS = 6


def padded(array, sides, width):
    for axis, dim in sides:
        peers, length = (lax.axis_size(axis), array.shape[dim])
        up = [(i, (i + 1) % peers) for i in range(peers)]
        down = [(j, i) for i, j in up]
        last = lax.slice_in_dim(array, length - width, length, axis=dim)
        initial = lax.slice_in_dim(array, 0, width, axis=dim)
        before = lax.ppermute(last, axis, up)
        after = lax.ppermute(initial, axis, down)
        array = jnp.concatenate([before, array, after], axis=dim)
    return array


def entering(value, axis, join, neutral):
    count, mine = (lax.axis_size(axis), lax.axis_index(axis))
    pieces = lax.all_gather(value, axis)
    pieces = pieces[::-1]
    mine = count - 1 - mine
    so_far = jnp.full_like(value, 0) + jnp.asarray(neutral, value.dtype)

    def hop(position, so_far):
        longer = join(so_far, pieces[position])
        return jnp.where(position < mine, longer, so_far)

    return lax.fori_loop(0, count - 1, hop, so_far)


def point_moments(centers, pert, weight, innov, places, radius):
    distance = jnp.abs(places[None, :] - centers[:, None])
    tapers = jnp.square(jnp.maximum(1.0 - distance / radius, 0.0)) * weight[None, :]
    scaled = (pert.astype(jnp.float32)[None] * tapers[:, None, :]).astype(jnp.bfloat16)
    gram_mats = jnp.einsum("gko,jo->gkj", scaled, pert, preferred_element_type=jnp.float32)
    drive_vec = jnp.einsum("gko,o->gk", scaled, innov, preferred_element_type=jnp.float32)
    return (gram_mats, drive_vec)


def chain_product(left_mats, right_mats):
    return jnp.einsum("pij,pjk->pik", left_mats, right_mats, precision=lax.Precision.HIGHEST)


def merge_pair(earlier, later):
    return chain_product(later, earlier)


def transform(gram_mats, drive_vec, members):
    identity = jnp.eye(members, dtype=jnp.float32)
    gram_mats = gram_mats + (members - 1.0) * identity
    norm_scale = jnp.sqrt(jnp.sum(gram_mats * gram_mats, axis=(1, 2)))
    upper_iter = gram_mats / norm_scale[:, None, None]
    lower_iter = jnp.broadcast_to(identity, gram_mats.shape)
    for sweep in range(NS_ITERS):
        middle = 1.5 * identity - 0.5 * chain_product(lower_iter, upper_iter)
        upper_iter = chain_product(upper_iter, middle)
        lower_iter = chain_product(middle, lower_iter)
    inv_root = lower_iter / jnp.sqrt(norm_scale)[:, None, None]
    inner = jnp.einsum("pij,pj->pi", inv_root, drive_vec, precision=lax.Precision.HIGHEST)
    mean_shift = jnp.einsum("pij,pj->pi", inv_root, inner, precision=lax.Precision.HIGHEST)
    full_weights = math.sqrt(members - 1.0) * inv_root + mean_shift[:, :, None]
    return full_weights - jnp.mean(full_weights, axis=1, keepdims=True) + 1.0 / members


def per_device(ensemble, obs_pert, obs_innov, obs_rinv, obs_tile, obs_column, obs_count):
    members = ensemble.shape[1]
    columns = ensemble.shape[2]
    own_obs = obs_pert.shape[2]
    tile_count = lax.axis_size("space")
    slot_size = max(2, 2 * own_obs // tile_count)
    recv_size = tile_count * slot_size
    radius = columns // 2
    points = columns // SPACING
    is_valid = jnp.arange(own_obs) < obs_count[0, 0]
    weight = jnp.where(is_valid, obs_rinv[0], jnp.zeros_like(obs_rinv[0]))
    destination = obs_tile[0, :, 0]
    dest_hits = (destination[:, None] == jnp.arange(tile_count)[None, :]).astype(jnp.int32)
    before = jnp.cumsum(dest_hits, axis=0) - dest_hits
    slot_rank = jnp.sum(before * dest_hits, axis=1)
    meta_rows = jnp.stack([weight, obs_innov[0]])
    placed = destination * slot_size + slot_rank
    send_pert = jnp.zeros((members, recv_size), jnp.bfloat16).at[:, placed].set(obs_pert[0])
    send_meta = jnp.zeros((2, recv_size), jnp.bfloat16).at[:, placed].set(meta_rows)
    send_cols = jnp.zeros((1, recv_size), jnp.int32).at[:, placed].set(obs_column)
    arrived = (
        lax.all_to_all(send_pert, "space", split_axis=1, concat_axis=1, tiled=True),
        lax.all_to_all(send_meta, "space", split_axis=1, concat_axis=1, tiled=True),
        lax.all_to_all(send_cols, "space", split_axis=1, concat_axis=1, tiled=True),
    )
    near_pert, near_meta, near_cols = (
        padded(arrived[0], (("space", 1),), recv_size),
        padded(arrived[1], (("space", 1),), recv_size),
        padded(arrived[2], (("space", 1),), recv_size),
    )
    offsets = jnp.repeat(jnp.array([-columns, 0, columns], dtype=jnp.int32), recv_size)
    places = (near_cols[0] + offsets).astype(jnp.float32)
    near_weight = near_meta[0].astype(jnp.float32)
    near_innov = near_meta[1]
    point_ids = jnp.arange(-1, points + 1)
    centers = (point_ids * SPACING + SPACING // 2).astype(jnp.float32)
    grouped = centers.reshape(-1, 2)

    def moments_of(pair_centers):
        return point_moments(pair_centers, near_pert, near_weight, near_innov, places, radius)

    gram_mats, drive_vec = lax.map(moments_of, grouped)
    gram_mats = gram_mats.reshape(-1, members, members)
    drive_vec = drive_vec.reshape(-1, members)
    weights_here = transform(gram_mats, drive_vec, members)
    identity = jnp.broadcast_to(jnp.eye(members, dtype=jnp.float32), weights_here.shape)
    suffix = entering(weights_here, "lag", merge_pair, identity)
    products = chain_product(weights_here, suffix)
    rounded = products.astype(jnp.bfloat16)
    half_span = SPACING // 2
    offsets_in = jnp.arange(SPACING).astype(jnp.float32)
    weight_mid = 1.0 - jnp.abs(offsets_in - half_span) / SPACING
    weight_prev = 1.0 - (offsets_in[:half_span] + half_span) / SPACING
    weight_next = 1.0 - (SPACING + half_span - offsets_in[half_span:]) / SPACING
    blocks = ensemble[0].reshape(members, points, SPACING)
    middle_part = jnp.einsum(
        "jkm,kjo->mjo", rounded[1 : points + 1], blocks, preferred_element_type=jnp.float32
    )
    lower_part = jnp.einsum(
        "jkm,kjo->mjo",
        rounded[0:points],
        blocks[:, :, :half_span],
        preferred_element_type=jnp.float32,
    )
    upper_part = jnp.einsum(
        "jkm,kjo->mjo",
        rounded[2 : points + 2],
        blocks[:, :, half_span:],
        preferred_element_type=jnp.float32,
    )
    sides = jnp.concatenate([lower_part * weight_prev, upper_part * weight_next], axis=2)
    analysed = middle_part * weight_mid + sides
    return analysed.reshape(1, members, columns).astype(jnp.bfloat16)


def solution(mesh):
    return jax.shard_map(
        per_device,
        mesh=mesh,
        in_specs=(
            P("lag", None, "space"),
            P("lag", None, "space"),
            P("lag", "space"),
            P("lag", "space"),
            P("lag", "space", None),
            P("lag", "space"),
            P("lag", "space"),
        ),
        out_specs=P("lag", None, "space"),
        check_vma=False,
    )
```

profile of v0, /device:TPU:1, one launch (start us, length us, event | category | flops | bytes accessed | tf_op | source)
XLA Modules:
  0.0 90.9 jit_solution(16204364311695344084)
XLA Ops:
  0.0 0.7 fusion.36
  0.7 4.5 %reduce-window.6 = s32[16,8,128]{2,1,0:T(8,128)S(1)} reduce-window(s32[16,8,128]{2,1,0:T(8,128)S(1)} %fusion.36, s32[]{:T(128)} %copy.90), window={size=1x1x128 pad=0_0x0_0x127_0}, to_apply=%region_0.1 | reduce-window | flops 2080768 | bytes 131076 | tf_op jit(solution)/shard_map/reduce-window
  5.6 0.7 fusion.35
  6.4 0.7 compare_select_fusion
  7.7 0.7 compare_select_fusion.1
  8.4 0.7 maximum_bitcast_fusion
  9.3 3.3 %scatter_custom_fusion.2 = bf16[2,2048]{0,1:T(8,128)(2,1)S(1)} fusion(s32[1024]{0:T(1024)S(1)} %bitcast.159, bf16[1024,2]{1,0:T(8,128)(2,1)S(1)} %copy.48, bf16[]{:T(256)} %constant.33.clone.1), kind=kCustom, calls=%fused_computation.50 | custom fusion | bytes 8194 | tf_op jit(solution)/shard_map/scatter | solution.py:91
  12.7 0.8 copy.49
  13.5 7.4 %all-to-all-start.2 = ((bf16[2,16,128]{2,0,1:T(2,128)(2,1)}), bf16[2,16,128]{2,0,1:T(2,128)(2,1)S(1)}, u32[]{:S(2)}, u32[]{:S(2)}) async-start(bf16[2,16,128]{2,0,1:T(2,128)(2,1)} %copy.49), calls=%async_computation.2 | async-start | bytes 16384 | tf_op jit(solution)/shard_map/all_to_all | solution.py:95
  21.0 5.0 %scatter_custom_fusion.1 = s32[2048]{0:T(1024)} fusion(s32[1024]{0:T(1024)S(1)} %bitcast.160, s32[1024]{0:T(1024)} %bitcast.162, s32[]{:T(128)} %copy.90), kind=kCustom, calls=%fused_computation.83 | custom fusion | bytes 8704 | tf_op jit(solution)/shard_map/scatter | solution.py:92
  26.0 1.0 %all-to-all-done.2 = bf16[2,16,128]{2,0,1:T(2,128)(2,1)S(1)} async-done(((bf16[2,16,128]{2,0,1:T(2,128)(2,1)}), bf16[2,16,128]{2,0,1:T(2,128)(2,1)S(1)}, u32[]{:S(2)}, u32[]{:S(2)}) %all-to-all-start.2) | async-done | bytes 8224 | tf_op jit(solution)/shard_map/all_to_all | solution.py:95
  27.0 5.4 %all-to-all-start.1 = ((s32[1,16,128]{2,0,1:T(1,128)}), s32[1,16,128]{2,0,1:T(1,128)S(1)}, u32[]{:S(2)}, u32[]{:S(2)}) async-start(s32[1,16,128]{2,0,1:T(1,128)} %bitcast.17), calls=%async_computation.1 | async-start | bytes 16384 | tf_op jit(solution)/shard_map/all_to_all | solution.py:96
  32.4 1.4 %collective-permute-start.4 = (bf16[2,2048]{1,0:T(2,128)(2,1)S(1)}, bf16[2,2048]{1,0:T(2,128)(2,1)S(1)}, u32[]{:S(2)}, u32[]{:S(2)}) collective-permute-start(bf16[2,2048]{1,0:T(2,128)(2,1)S(1)} %bitcast.149), channel_id=1, source_target_pairs={{0,1},{1,2},{2,3},{3,4},{4,5},{5,6},{6,7},{7,8},{8,9},{9,10},{10,1... | collective-permute-start | bytes 24584 | tf_op jit(solution)/shard_map/ppermute | solution.py:19
  33.8 3.7 %collective-permute-start.5 = (bf16[2,2048]{1,0:T(2,128)(2,1)S(1)}, bf16[2,2048]{1,0:T(2,128)(2,1)S(1)}, u32[]{:S(2)}, u32[]{:S(2)}) collective-permute-start(bf16[2,2048]{1,0:T(2,128)(2,1)S(1)} %bitcast.150), channel_id=1, source_target_pairs={{1,0},{2,1},{3,2},{4,3},{5,4},{6,5},{7,6},{8,7},{9,8},{10,9},{11,1... | collective-permute-start | bytes 24584 | tf_op jit(solution)/shard_map/ppermute | solution.py:20
  37.7 3.3 %scatter_custom_fusion = bf16[64,2048]{0,1:T(8,128)(2,1)S(1)} fusion(s32[1024]{0:T(1024)S(1)} %bitcast.161, bf16[1024,64]{1,0:T(8,128)(2,1)S(1)} %copy.45, bf16[]{:T(256)} %constant.33.clone.1), kind=kCustom, calls=%fused_computation.52 | custom fusion | bytes 262146 | tf_op jit(solution)/shard_map/scatter | solution.py:90
  41.0 0.9 copy.46
  42.4 3.5 %all-to-all-start = ((bf16[64,16,128]{2,0,1:T(8,128)(2,1)}), bf16[64,16,128]{2,0,1:T(8,128)(2,1)S(1)}, u32[]{:S(2)}, u32[]{:S(2)}) async-start(bf16[64,16,128]{2,0,1:T(8,128)(2,1)} %copy.46), calls=%async_computation | async-start | bytes 524288 | tf_op jit(solution)/shard_map/all_to_all | solution.py:94
  46.0 1.2 %collective-permute-start.2 = (s32[1,2048]{1,0:T(1,128)S(1)}, s32[1,2048]{1,0:T(1,128)S(1)}, u32[]{:S(2)}, u32[]{:S(2)}) collective-permute-start(s32[1,2048]{1,0:T(1,128)S(1)} %bitcast.152), channel_id=1, source_target_pairs={{0,1},{1,2},{2,3},{3,4},{4,5},{5,6},{6,7},{7,8},{8,9},{9,10},{10,1... | collective-permute-start | bytes 24584 | tf_op jit(solution)/shard_map/ppermute | solution.py:19
  47.2 3.9 %collective-permute-start.3 = (s32[1,2048]{1,0:T(1,128)S(1)}, s32[1,2048]{1,0:T(1,128)S(1)}, u32[]{:S(2)}, u32[]{:S(2)}) collective-permute-start(s32[1,2048]{1,0:T(1,128)S(1)} %bitcast.153), channel_id=1, source_target_pairs={{1,0},{2,1},{3,2},{4,3},{5,4},{6,5},{7,6},{8,7},{9,8},{10,9},{11,1... | collective-permute-start | bytes 24584 | tf_op jit(solution)/shard_map/ppermute | solution.py:20
  51.1 3.1 %collective-permute-done.2 = s32[1,2048]{1,0:T(1,128)S(1)} collective-permute-done((s32[1,2048]{1,0:T(1,128)S(1)}, s32[1,2048]{1,0:T(1,128)S(1)}, u32[]{:S(2)}, u32[]{:S(2)}) %collective-permute-start.2) | collective-permute-done | bytes 8224 | tf_op jit(solution)/shard_map/ppermute | solution.py:19
  54.5 4.9 %collective-permute-start.1 = (bf16[64,2048]{1,0:T(8,128)(2,1)S(1)}, bf16[64,2048]{1,0:T(8,128)(2,1)S(1)}, u32[]{:S(2)}, u32[]{:S(2)}) collective-permute-start(bf16[64,2048]{1,0:T(8,128)(2,1)S(1)} %copy_bitcast_fusion), channel_id=1, source_target_pairs={{1,0},{2,1},{3,2},{4,3},{5,4},{6,5},{7,6},{8,7},{9,8},{10,9},{11,1... | collective-permute-start | bytes 786440 | tf_op jit(solution)/shard_map/ppermute | solution.py:20
  59.5 3.8 %collective-permute-done = bf16[64,2048]{1,0:T(8,128)(2,1)S(1)} collective-permute-done((bf16[64,2048]{1,0:T(8,128)(2,1)S(1)}, bf16[64,2048]{1,0:T(8,128)(2,1)S(1)}, u32[]{:S(2)}, u32[]{:S(2)}) %collective-permute-start) | collective-permute-done | bytes 262176 | tf_op jit(solution)/shard_map/ppermute | solution.py:19
  63.4 8.0 %while.2 = (s32[]{:T(128)}, f32[5,2,64,64]{3,2,1,0:T(8,128)S(1)}, f32[5,2,64]{2,1,0:T(2,128)S(1)}, bf16[64,6144]{1,0:T(8,128)(2,1)S(1)}, f32[6144]{0:T(1024)S(1)...) while((s32[]{:T(128)}, f32[5,2,64,64]{3,2,1,0:T(8,128)S(1)}, ...), condition=%wide.region_7.8_spmd, body=%wide.region_6.7_spmd.sunk | while | flops 105861120 | bytes 6593153 | solution.py:114
  63.7 0.6 fusion.106
  64.3 0.7 fusion.107
  65.3 0.6 fusion.106
  65.9 0.7 fusion.107
  66.9 0.6 fusion.106
  67.5 0.7 fusion.107
  68.5 0.6 fusion.106
  69.1 0.7 fusion.107
  70.1 0.6 fusion.106
  70.7 0.7 fusion.107
  72.2 0.5 fusion.45
  73.1 0.5 fusion.16
  73.6 0.5 fusion.47
  74.0 0.5 fusion.46
  74.5 0.5 fusion.17
  74.9 0.5 fusion.49
  75.9 0.5 fusion.18
  77.3 0.5 fusion.19
  78.7 0.5 fusion.20
  79.1 0.5 convolution_divide_fusion
  79.6 0.6 fusion.54
  80.2 0.6 fusion.40
  81.2 6.6 %all-gather = f32[20,64,64]{2,1,0:T(8,128)S(1)} all-gather(f32[10,64,64]{2,1,0:T(8,128)S(1)} %subtract_add_fusion), channel_id=2, replica_groups=mesh['lag'=2,'space'=16] {'lag'}, dimensions={0}, use_global_device_ids=true | all-gather | bytes 491520 | tf_op jit(solution)/shard_map/all_gather | solution.py:27
  88.2 0.5 convolution_convert_fusion
  89.9 1.0 %convert_element_type.78 = bf16[1,64,4096]{2,1,0:T(8,128)(2,1)} reshape(bf16[64,8,512]{2,1,0:T(8,128)(2,1)S(1)} %copy.56) | data formatting | bytes 1048576 | tf_op jit(solution)/shard_map/convert_element_type | solution.py:145
  (87 shorter events, 8.5 us)
Async XLA Ops:
  0.0 37.5 %copy-start.1 = (bf16[1,64,1024]{2,1,0:T(8,128)(2,1)S(1)}, bf16[1,64,1024]{2,1,0:T(8,128)(2,1)}, u32[]{:S(2)}) copy-start(bf16[1,64,1024]{2,1,0:T(8,128)(2,1)} %param.11) | copy-start | bytes 393220
  9.1 32.8 %copy-start.2 = (s32[3]{0:T(128)S(1)}, s32[3]{0:T(128)}, u32[]{:S(2)}) copy-start(s32[3]{0:T(128)} %constant.94.clone) | copy-start | bytes 40
  9.3 32.7 %copy-start = (bf16[1,64,4096]{2,1,0:T(8,128)(2,1)S(1)}, bf16[1,64,4096]{2,1,0:T(8,128)(2,1)}, u32[]{:S(2)}) copy-start(bf16[1,64,4096]{2,1,0:T(8,128)(2,1)} %param.10) | copy-start | bytes 1572868
  13.5 13.5 %all-to-all-start.2 = ((bf16[2,16,128]{2,0,1:T(2,128)(2,1)}), bf16[2,16,128]{2,0,1:T(2,128)(2,1)S(1)}, u32[]{:S(2)}, u32[]{:S(2)}) async-start(bf16[2,16,128]{2,0,1:T(2,128)(2,1)} %copy.49), calls=%async_computation.2 | async-start | bytes 16384 | tf_op jit(solution)/shard_map/all_to_all | solution.py:95
  27.0 15.4 %all-to-all-start.1 = ((s32[1,16,128]{2,0,1:T(1,128)}), s32[1,16,128]{2,0,1:T(1,128)S(1)}, u32[]{:S(2)}, u32[]{:S(2)}) async-start(s32[1,16,128]{2,0,1:T(1,128)} %bitcast.17), calls=%async_computation.1 | async-start | bytes 16384 | tf_op jit(solution)/shard_map/all_to_all | solution.py:96
  32.4 18.7 %collective-permute-start.4 = (bf16[2,2048]{1,0:T(2,128)(2,1)S(1)}, bf16[2,2048]{1,0:T(2,128)(2,1)S(1)}, u32[]{:S(2)}, u32[]{:S(2)}) collective-permute-start(bf16[2,2048]{1,0:T(2,128)(2,1)S(1)} %bitcast.149), channel_id=1, source_target_pairs={{0,1},{1,2},{2,3},{3,4},{4,5},{5,6},{6,7},{7,8},{8,9},{9,10},{10,1... | collective-permute-start | bytes 24584 | tf_op jit(solution)/shard_map/ppermute | solution.py:19
  33.8 17.3 %collective-permute-start.5 = (bf16[2,2048]{1,0:T(2,128)(2,1)S(1)}, bf16[2,2048]{1,0:T(2,128)(2,1)S(1)}, u32[]{:S(2)}, u32[]{:S(2)}) collective-permute-start(bf16[2,2048]{1,0:T(2,128)(2,1)S(1)} %bitcast.150), channel_id=1, source_target_pairs={{1,0},{2,1},{3,2},{4,3},{5,4},{6,5},{7,6},{8,7},{9,8},{10,9},{11,1... | collective-permute-start | bytes 24584 | tf_op jit(solution)/shard_map/ppermute | solution.py:20
  42.4 11.8 %all-to-all-start = ((bf16[64,16,128]{2,0,1:T(8,128)(2,1)}), bf16[64,16,128]{2,0,1:T(8,128)(2,1)S(1)}, u32[]{:S(2)}, u32[]{:S(2)}) async-start(bf16[64,16,128]{2,0,1:T(8,128)(2,1)} %copy.46), calls=%async_computation | async-start | bytes 524288 | tf_op jit(solution)/shard_map/all_to_all | solution.py:94
  46.0 8.3 %collective-permute-start.2 = (s32[1,2048]{1,0:T(1,128)S(1)}, s32[1,2048]{1,0:T(1,128)S(1)}, u32[]{:S(2)}, u32[]{:S(2)}) collective-permute-start(s32[1,2048]{1,0:T(1,128)S(1)} %bitcast.152), channel_id=1, source_target_pairs={{0,1},{1,2},{2,3},{3,4},{4,5},{5,6},{6,7},{7,8},{8,9},{9,10},{10,1... | collective-permute-start | bytes 24584 | tf_op jit(solution)/shard_map/ppermute | solution.py:19
  47.2 7.0 %collective-permute-start.3 = (s32[1,2048]{1,0:T(1,128)S(1)}, s32[1,2048]{1,0:T(1,128)S(1)}, u32[]{:S(2)}, u32[]{:S(2)}) collective-permute-start(s32[1,2048]{1,0:T(1,128)S(1)} %bitcast.153), channel_id=1, source_target_pairs={{1,0},{2,1},{3,2},{4,3},{5,4},{6,5},{7,6},{8,7},{9,8},{10,9},{11,1... | collective-permute-start | bytes 24584 | tf_op jit(solution)/shard_map/ppermute | solution.py:20
  54.3 9.0 %collective-permute-start = (bf16[64,2048]{1,0:T(8,128)(2,1)S(1)}, bf16[64,2048]{1,0:T(8,128)(2,1)S(1)}, u32[]{:S(2)}, u32[]{:S(2)}) collective-permute-start(bf16[64,2048]{1,0:T(8,128)(2,1)S(1)} %copy_bitcast_fusion), channel_id=1, source_target_pairs={{0,1},{1,2},{2,3},{3,4},{4,5},{5,6},{6,7},{7,8},{8,9},{9,10},{10,1... | collective-permute-start | bytes 786440 | tf_op jit(solution)/shard_map/ppermute | solution.py:19
  54.5 8.8 %collective-permute-start.1 = (bf16[64,2048]{1,0:T(8,128)(2,1)S(1)}, bf16[64,2048]{1,0:T(8,128)(2,1)S(1)}, u32[]{:S(2)}, u32[]{:S(2)}) collective-permute-start(bf16[64,2048]{1,0:T(8,128)(2,1)S(1)} %copy_bitcast_fusion), channel_id=1, source_target_pairs={{1,0},{2,1},{3,2},{4,3},{5,4},{6,5},{7,6},{8,7},{9,8},{10,9},{11,1... | collective-permute-start | bytes 786440 | tf_op jit(solution)/shard_map/ppermute | solution.py:20
where the time goes:
time: 91.8 us; the launch traced here: 90.9 us
  starting transfers between devices  31.7 us (35%)
  matrix products  17.2 us (19%)
  local copies, waits for them, and re-layouts  16.2 us (18%)
  other arithmetic  10.1 us (11%)
  waiting for transfers between devices  7.93 us (9%)
  blocking collectives  6.55 us (7%)
  between operations  1.06 us (1%)
    ppermute x3, starting transfers between devices, padded(): after = lax.ppermute(initial, axis, down)  12.5 us
    dot_general x19, matrix products, chain_product(): jnp.einsum('pij,pjk->pik', left_mats, right_mats, precision=lax.Precision...  8.53 us
    all_to_all x1, starting transfers between devices, per_device(): lax.all_to_all(send_meta, 'space', split_axis=1, concat_axis=1, tiled=True)  7.4 us
    ppermute x3, waiting for transfers between devices, padded(): before = lax.ppermute(last, axis, up)  6.89 us
    all_gather x1, blocking collectives, entering(): pieces = lax.all_gather(value, axis)  6.55 us
    all_to_all x1, starting transfers between devices, per_device(): lax.all_to_all(send_cols, 'space', split_axis=1, concat_axis=1, tiled=True)  5.39 us
    scatter x1, local copies, waits for them, and re-layouts, per_device(): jnp.zeros((1, recv_size), jnp.int32).at[:, placed].set(obs_column)  5.04 us
    another operation x3, other arithmetic  4.61 us
  transfers between devices with their start and end apart: 9, of which 4 were waited for; matrix products, arithmetic and copies ran while one was open for 11% of the time, Pallas kernels for 0%

commit v1 on v0

v1 whole, which is shorter than its diff:
```python
import functools
import math

import jax
import jax.numpy as jnp
from jax import lax
from jax.experimental import pallas as pl
from jax.experimental.pallas import tpu as pltpu
from jax.sharding import PartitionSpec as P

SPACING = 512
NS_ITERS = 6
LANES = 128
META = 16
BASE = 64
F32 = jnp.float32
BF16 = jnp.bfloat16
NT = (((1,), (1,)), ((), ()))


def halves(x):
    hi = x.astype(BF16)
    return hi, (x - hi.astype(F32)).astype(BF16)


def stationary(hi, lo):
    row = jnp.concatenate([hi, lo], axis=1)
    return jnp.concatenate([row, row], axis=0)


def times(left, weights):
    width = weights.shape[1] // 2
    hi, lo = halves(left)
    out = jnp.dot(jnp.concatenate([hi, lo], axis=1), weights, preferred_element_type=F32)
    return out[:, :width] + out[:, width:]


def weights_kernel(
    tiles, lags, slots, group, columns,
    pert_ref, innov_ref, rinv_ref, tile_ref, col_ref, count_ref,
    out_ref,
    msg, snd, rcv, acc, to_left, to_right, from_left, from_right, mine, theirs,
    a2a_send, a2a_recv, halo_send, halo_recv, lag_send, lag_recv,
):
    members, own = pert_ref.shape
    points = columns // SPACING
    half = points // 2
    radius = columns // 2
    pair = 2 * members
    me = lax.axis_index("space")
    my_lag = lax.axis_index("lag")

    barrier = pltpu.get_barrier_semaphore()
    for step in range(1, tiles):
        pl.semaphore_signal(barrier, inc=1, device_id={"space": lax.rem(me + step, tiles)})
    for step in range(1, lags):
        pl.semaphore_signal(barrier, inc=1, device_id={"lag": lax.rem(my_lag + step, lags)})

    slot_id = lax.broadcasted_iota(jnp.int32, (1, own), 1)
    weight = jnp.where(slot_id < count_ref[0, 0], rinv_ref[...].astype(F32), 0.0)
    column = col_ref[...]
    col_hi = (column // BASE).astype(F32)
    col_lo = (column % BASE).astype(F32)
    row = lax.broadcasted_iota(jnp.int32, (META, own), 0)
    meta = jnp.where(row == 0, weight, 0.0)
    meta = jnp.where(row == 1, innov_ref[...].astype(F32), meta)
    meta = jnp.where(row == 2, col_hi, meta)
    meta = jnp.where(row == 3, col_lo, meta)
    msg[0:members, :] = pert_ref[...]
    msg[members:, :] = meta.astype(BF16)

    target = tile_ref[...]
    hits = jnp.where(target == lax.broadcasted_iota(jnp.int32, (tiles, own), 0), 1.0, 0.0)
    tri = jnp.where(
        lax.broadcasted_iota(jnp.int32, (LANES, LANES), 0)
        < lax.broadcasted_iota(jnp.int32, (LANES, LANES), 1),
        1.0, 0.0,
    ).astype(BF16)
    seen = jnp.zeros((tiles, 1), F32)
    ranks = []
    for b in range(own // LANES):
        block = hits[:, b * LANES : (b + 1) * LANES]
        ahead = jnp.dot(block.astype(BF16), tri, preferred_element_type=F32) + seen
        ranks.append(jnp.sum(ahead * block, axis=0, keepdims=True))
        seen = seen + jnp.sum(block, axis=1, keepdims=True)
    rank = jnp.concatenate(ranks, axis=1).astype(jnp.int32)
    key = target * slots + rank
    place = lax.broadcasted_iota(jnp.int32, (slots, own), 0)
    message = msg[...]

    def bucket(dest):
        chosen = jnp.where(place == key - dest * slots, 1.0, 0.0).astype(BF16)
        return lax.dot_general(message, chosen, NT, preferred_element_type=F32).astype(BF16)

    def a2a(step):
        return pltpu.make_async_remote_copy(
            src_ref=snd.at[step], dst_ref=rcv.at[step],
            send_sem=a2a_send.at[step], recv_sem=a2a_recv.at[step],
            device_id={"space": lax.rem(me + step, tiles)},
        )

    for step in range(1, tiles):
        snd[step] = bucket(lax.rem(me + step, tiles))
        if step == 1:
            pl.semaphore_wait(barrier, tiles - 1 + lags - 1)
        else:
            a2a(step - 1).start()
    rcv[0] = bucket(me)
    a2a(tiles - 1).start()

    for first in range(0, tiles, group):
        for step in range(max(first, 1), first + group):
            a2a(step).wait_recv()
        obs = jnp.concatenate([rcv[step] for step in range(first, first + group)], axis=1)
        pert = obs[0:members].astype(F32)
        info = obs[members:].astype(F32)
        obs_weight = info[0:1]
        places = info[2:3] * BASE + info[3:4]
        for k in range(points + 2 * half):
            center = float((k - half) * SPACING + SPACING // 2)
            taper = jnp.maximum(1.0 - jnp.abs(places - center) / radius, 0.0)
            rho = taper * taper * obs_weight
            scaled = (pert * rho).astype(BF16)
            part = lax.dot_general(scaled, obs, NT, preferred_element_type=F32)
            if first == 0:
                acc[k] = part
            else:
                acc[k] += part

    lane = lax.broadcasted_iota(jnp.int32, (members, pair), 1)
    low = lane < members

    def joined(a, b):
        return jnp.concatenate([acc[a, :, 0:members], acc[b, :, 0:members]], axis=1)

    def drive_of(a):
        return acc[a, :, members + 1 : members + 2]

    pairs_side = (half + 2) // 2
    last = points + 2 * half - 1
    left_own = jnp.concatenate([jnp.zeros((members, members), F32), acc[0, :, 0:members]], axis=1)
    for j in range(half + 1):
        left_own = jnp.where(lane == j, drive_of(j), left_own)
    to_left[0] = left_own
    for i in range(1, pairs_side):
        to_left[i] = joined(2 * i - 1, 2 * i)
    right_own = jnp.concatenate([acc[last, :, 0:members], jnp.zeros((members, members), F32)], axis=1)
    for j in range(half + 1):
        right_own = jnp.where(lane == members + j, drive_of(last - half + j), right_own)
    to_right[pairs_side - 1] = right_own
    for i in range(pairs_side - 1):
        to_right[i] = joined(last - half + 2 * i, last - half + 2 * i + 1)

    eye = jnp.where(
        lax.rem(lane, members) == lax.broadcasted_iota(jnp.int32, (members, pair), 0), 1.0, 0.0
    )
    mask_low = jnp.where(low, 1.0, 0.0).astype(BF16)
    mask_high = jnp.where(low, 0.0, 1.0).astype(BF16)

    def diagonal(x):
        return jnp.concatenate([x * mask_low, x * mask_high], axis=0)

    def blocks(x):
        hi, lo = halves(x)
        return stationary(diagonal(hi), diagonal(lo))

    left_copy = pltpu.make_async_remote_copy(
        src_ref=to_left, dst_ref=from_right, send_sem=halo_send.at[0], recv_sem=halo_recv.at[0],
        device_id={"space": lax.rem(me + tiles - 1, tiles)},
    )
    right_copy = pltpu.make_async_remote_copy(
        src_ref=to_right, dst_ref=from_left, send_sem=halo_send.at[1], recv_sem=halo_recv.at[1],
        device_id={"space": lax.rem(me + 1, tiles)},
    )
    left_copy.start()
    right_copy.start()

    count = (points + 2) // 2
    own_pairs = [joined(half - 1 + 2 * i, half + 2 * i) for i in range(count)]
    own_drives = [drive_of(half - 1 + j) for j in range(points + 2)]
    left_copy.wait_recv()
    right_copy.wait_recv()
    lefts = [from_left[i] for i in range(pairs_side)]
    rights = [from_right[i] for i in range(pairs_side)]

    grams, drives = [], []
    for i in range(count):
        total = own_pairs[i] + (members - 1.0) * eye
        if i < pairs_side - 1:
            total = total + lefts[i]
        elif i == pairs_side - 1:
            total = total + jnp.where(low, lefts[i], rights[0])
        else:
            total = total + rights[i - pairs_side + 1]
        grams.append(total)
    for j in range(points + 2):
        if j <= half:
            other = lefts[pairs_side - 1][:, members + j : members + j + 1]
        else:
            other = rights[0][:, j - half - 1 : j - half]
        drives.append(own_drives[j] + other)

    uppers, lowers, scales = [], [], []
    for total in grams:
        squares = jnp.sum(total * total, axis=0, keepdims=True)
        row_low = lax.broadcasted_iota(jnp.int32, (1, pair), 1) < members
        sum_low = jnp.sum(jnp.where(row_low, squares, 0.0), axis=1, keepdims=True)
        sum_high = jnp.sum(jnp.where(row_low, 0.0, squares), axis=1, keepdims=True)
        scale = jnp.sqrt(jnp.where(row_low, sum_low, sum_high))
        scales.append(scale)
        uppers.append(total / scale)

    for sweep in range(NS_ITERS):
        if sweep == 0:
            middles = [1.5 * eye - 0.5 * up for up in uppers]
            lowers = middles
            uppers = [times(up, blocks(mid)) for up, mid in zip(uppers, middles)]
        else:
            middles = [
                1.5 * eye - 0.5 * times(lo, blocks(up)) for lo, up in zip(lowers, uppers)
            ]
            if sweep < NS_ITERS - 1:
                both = [
                    times(jnp.concatenate([up, lo], axis=0), blocks(mid))
                    for up, lo, mid in zip(uppers, lowers, middles)
                ]
                uppers = [x[0:members] for x in both]
                lowers = [x[members:] for x in both]
            else:
                lowers = [times(lo, blocks(mid)) for lo, mid in zip(lowers, middles)]

    results = []
    for i in range(count):
        root = lowers[i] / jnp.sqrt(scales[i])
        top = jnp.where(low, drives[2 * i], 0.0)
        bottom = jnp.where(low, 0.0, drives[2 * i + 1])
        hi, lo = halves(jnp.concatenate([top, bottom], axis=0))
        inner = times(root, stationary(hi, lo))
        shift = times(root, blocks(inner))
        full = math.sqrt(members - 1.0) * root + shift
        results.append(full - jnp.mean(full, axis=0, keepdims=True) + 1.0 / members)
    for i in range(count):
        mine[i] = results[i]

    def lag_copy(step):
        return pltpu.make_async_remote_copy(
            src_ref=mine, dst_ref=theirs.at[step - 1],
            send_sem=lag_send.at[step - 1], recv_sem=lag_recv.at[step - 1],
            device_id={"lag": lax.rem(my_lag + lags - step, lags)},
        )

    for step in range(1, lags):
        lag_copy(step).start()
    for step in range(1, lags):
        lag_copy(step).wait_recv()
        later = my_lag + step < lags
        for i in range(count):
            longer = times(results[i], blocks(theirs[step - 1, i]))
            results[i] = jnp.where(later, longer, results[i])
    for i in range(count):
        out_ref[i] = results[i].astype(BF16)

    for step in range(1, tiles):
        a2a(step).wait_send()
    left_copy.wait_send()
    right_copy.wait_send()
    for step in range(1, lags):
        lag_copy(step).wait_send()


def apply_kernel(members, columns, weights_ref, ens_ref, out_ref):
    points = columns // SPACING
    turned = jnp.concatenate(
        [weights_ref[i].astype(F32).T.astype(BF16) for i in range((points + 2) // 2)], axis=0
    )
    half_span = SPACING // 2
    for s in range(points + 1):
        start = max(s * SPACING - half_span, 0)
        stop = min(s * SPACING + half_span, columns)
        both = jnp.dot(
            turned[s * members : (s + 2) * members], ens_ref[:, start:stop],
            preferred_element_type=F32,
        )
        along = lax.broadcasted_iota(jnp.int32, (1, stop - start), 1).astype(F32)
        second = (along + float(start - (s * SPACING - half_span))) / SPACING
        mixed = both[0:members] * (1.0 - second) + both[members:] * second
        out_ref[:, start:stop] = mixed.astype(BF16)


def per_device(ensemble, obs_pert, obs_innov, obs_rinv, obs_tile, obs_column, obs_count):
    members, columns = ensemble.shape[1:]
    own = obs_pert.shape[2]
    tiles, lags = lax.axis_size("space"), lax.axis_size("lag")
    slot_size = max(2, 2 * own // tiles)
    slots = -(-slot_size // LANES) * LANES
    group = 4
    points = columns // SPACING
    half = points // 2
    count = (points + 2) // 2
    pair = 2 * members
    rows = members + META
    side = ((half + 2) // 2, members, pair)
    vmem = pl.BlockSpec(memory_space=pltpu.VMEM)
    products = pl.pallas_call(
        functools.partial(weights_kernel, tiles, lags, slots, group, columns),
        out_shape=jax.ShapeDtypeStruct((count, members, pair), BF16),
        in_specs=[vmem] * 5 + [pl.BlockSpec(memory_space=pltpu.SMEM)],
        out_specs=vmem,
        scratch_shapes=[
            pltpu.VMEM((rows, own), BF16),
            pltpu.VMEM((tiles, rows, slots), BF16),
            pltpu.VMEM((tiles, rows, slots), BF16),
            pltpu.VMEM((points + 2 * half, members, rows), F32),
            pltpu.VMEM(side, F32),
            pltpu.VMEM(side, F32),
            pltpu.VMEM(side, F32),
            pltpu.VMEM(side, F32),
            pltpu.VMEM((count, members, pair), F32),
            pltpu.VMEM((max(lags - 1, 1), count, members, pair), F32),
            pltpu.SemaphoreType.DMA((tiles,)),
            pltpu.SemaphoreType.DMA((tiles,)),
            pltpu.SemaphoreType.DMA((2,)),
            pltpu.SemaphoreType.DMA((2,)),
            pltpu.SemaphoreType.DMA((max(lags - 1, 1),)),
            pltpu.SemaphoreType.DMA((max(lags - 1, 1),)),
        ],
        compiler_params=pltpu.CompilerParams(collective_id=0, has_side_effects=True),
        name="ensemble_weights",
    )(obs_pert[0], obs_innov, obs_rinv, obs_tile[:, :, 0], obs_column, obs_count)
    analysis = pl.pallas_call(
        functools.partial(apply_kernel, members, columns),
        out_shape=jax.ShapeDtypeStruct((members, columns), BF16),
        in_specs=[vmem] * 2,
        out_specs=vmem,
        name="apply_weights",
    )(products, ensemble[0])
    return analysis[None]


def solution(mesh):
    return jax.shard_map(
        per_device,
        mesh=mesh,
        in_specs=(
            P("lag", None, "space"),
            P("lag", None, "space"),
            P("lag", "space"),
            P("lag", "space"),
            P("lag", "space", None),
            P("lag", "space"),
            P("lag", "space"),
        ),
        out_specs=P("lag", None, "space"),
        check_vma=False,
    )
```

time: 91.8 us -> 32.3 us (0.35)
  starting transfers between devices: 31.7 us -> 0 us
  Pallas kernels: 0 us -> 31.4 us
  matrix products: 17.2 us -> 0 us
  local copies, waits for them, and re-layouts: 16.2 us -> 0 us
  other arithmetic: 10.1 us -> 0 us
  waiting for transfers between devices: 7.93 us -> 0 us
  blocking collectives: 6.55 us -> 0 us
    pallas_call x0 -> x2, Pallas kernels: none -> 31.4 us  [the longest x1 29.1 us: per_device(): pl.pallas_call(functools.partial(weights_kernel, tiles, lags, slots, grou...]
    dot_general x34 -> x0, matrix products: 17.2 us -> none  [the longest x19 8.53 us: chain_product(): jnp.einsum('pij,pjk->pik', left_mats, right_mats, precision=lax.Precision...]
    all_to_all x3 -> x0, starting transfers between devices: 16.3 us -> none  [the longest x1 7.4 us: per_device(): lax.all_to_all(send_meta, 'space', split_axis=1, concat_axis=1, tiled=True)]
    ppermute x6 -> x0, starting transfers between devices: 15.3 us -> none  [the longest x3 12.5 us: padded(): after = lax.ppermute(initial, axis, down)]
    scatter x3 -> x0, local copies, waits for them, and re-layouts: 11.7 us -> none  [the longest x1 5.04 us: per_device(): jnp.zeros((1, recv_size), jnp.int32).at[:, placed].set(obs_column)]
    ppermute x6 -> x0, waiting for transfers between devices: 6.98 us -> none  [the longest x3 6.89 us: padded(): before = lax.ppermute(last, axis, up)]
    all_gather x1 -> x0, blocking collectives: 6.55 us -> none  [entering(): pieces = lax.all_gather(value, axis)]
    another operation x4 -> x0, other arithmetic: 5.31 us -> none
  transfers between devices with their start and end apart: 9 -> 0, of which waited for: 4 -> 0; matrix products, arithmetic and copies ran while one was open for 11% -> 0% of each run, Pallas kernels for 0% -> 0%
where the time goes in v1:
time: 32.3 us; the launch traced here: 32.1 us
  Pallas kernels  31.4 us (97%)
  between operations  0.66 us (2%)
    pallas_call x1, Pallas kernels, per_device(): pl.pallas_call(functools.partial(weights_kernel, tiles, lags, slots, grou...  29.1 us
    pallas_call x1, Pallas kernels, per_device(): pl.pallas_call(functools.partial(apply_kernel, members, columns), out_sha...  2.38 us

profile of v1, /device:TPU:1, one launch (start us, length us, event | category | flops | bytes accessed | tf_op | source)
XLA Modules:
  0.0 32.1 jit_solution(17927146779678973352)
XLA Ops:
  0.7 29.1 %ensemble_weights.1.weights_ref = bf16[5,64,128]{2,1,0:T(8,128)(2,1)} custom-call(bf16[64,1024]{1,0:T(8,128)(2,1)} %bitcast.5, bf16[1,1024]{1,0:T(2,128)(2,1)} %innov_ref.1, bf16[1,1024]{1,0:T(2,128)(2,1)} %rinv_ref.1, s32[1,1024]{1,0:T(1,128)} %bitcast.6, s32[1,1024]{1,0:T(1,128)} %col_ref.1, s32[1,1]{1,0:T(1,128)S(6)} %copy.8.count_ref), custom_call_target="tpu_custom_call" | custom-call | tf_op jit(solution)/shard_map/ensemble_weights/pallas_call | solution.py:304
  29.7 2.4 %apply_weights.1 = bf16[64,4096]{1,0:T(8,128)(2,1)} custom-call(bf16[5,64,128]{2,1,0:T(8,128)(2,1)} %ensemble_weights.1.weights_ref, bf16[64,4096]{1,0:T(8,128)(2,1)} %bitcast.4), custom_call_target="tpu_custom_call" | custom-call | tf_op jit(solution)/shard_map/apply_weights/pallas_call | solution.py:330

commit v2 on v1

--- a/solution.py
+++ b/solution.py
@@ -37,24 +37,44 @@
 
 def weights_kernel(
     tiles, lags, slots, group, columns,
-    pert_ref, innov_ref, rinv_ref, tile_ref, col_ref, count_ref,
-    out_ref,
+    pert_hbm, innov_hbm, rinv_hbm, tile_hbm, col_hbm, count_hbm, ens_hbm,
+    out_hbm,
+    ens, out, move_sem,
+    innov_ref, rinv_ref, tile_ref, col_ref, count_ref, load_sem,
     msg, snd, rcv, acc, to_left, to_right, from_left, from_right, mine, theirs,
     a2a_send, a2a_recv, halo_send, halo_recv, lag_send, lag_recv,
 ):
-    members, own = pert_ref.shape
+    members, own = pert_hbm.shape
     points = columns // SPACING
     half = points // 2
     radius = columns // 2
     pair = 2 * members
+    sent = members + META // 2
     me = lax.axis_index("space")
     my_lag = lax.axis_index("lag")
 
     barrier = pltpu.get_barrier_semaphore()
-    for step in range(1, tiles):
+    order = range(tiles - 1, 0, -1)
+    for step in order:
         pl.semaphore_signal(barrier, inc=1, device_id={"space": lax.rem(me + step, tiles)})
     for step in range(1, lags):
         pl.semaphore_signal(barrier, inc=1, device_id={"lag": lax.rem(my_lag + step, lags)})
+
+    loads = [
+        pltpu.make_async_copy(source, dest, load_sem.at[n])
+        for n, (source, dest) in enumerate((
+            (tile_hbm, tile_ref),
+            (count_hbm, count_ref),
+            (rinv_hbm, rinv_ref),
+            (innov_hbm, innov_ref),
+            (col_hbm, col_ref),
+            (pert_hbm, msg.at[0:members]),
+        ))
+    ]
+    for load in loads:
+        load.start()
+    for load in loads:
+        load.wait()
 
     slot_id = lax.broadcasted_iota(jnp.int32, (1, own), 1)
     weight = jnp.where(slot_id < count_ref[0, 0], rinv_ref[...].astype(F32), 0.0)
@@ -66,7 +86,6 @@
     meta = jnp.where(row == 1, innov_ref[...].astype(F32), meta)
     meta = jnp.where(row == 2, col_hi, meta)
     meta = jnp.where(row == 3, col_lo, meta)
-    msg[0:members, :] = pert_ref[...]
     msg[members:, :] = meta.astype(BF16)
 
     target = tile_ref[...]
@@ -94,38 +113,46 @@
 
     def a2a(step):
         return pltpu.make_async_remote_copy(
-            src_ref=snd.at[step], dst_ref=rcv.at[step],
+            src_ref=snd.at[step, 0:sent], dst_ref=rcv.at[step, 0:sent],
             send_sem=a2a_send.at[step], recv_sem=a2a_recv.at[step],
             device_id={"space": lax.rem(me + step, tiles)},
         )
 
-    for step in range(1, tiles):
+    for step in order:
         snd[step] = bucket(lax.rem(me + step, tiles))
-        if step == 1:
-            pl.semaphore_wait(barrier, tiles - 1 + lags - 1)
-        else:
-            a2a(step - 1).start()
     rcv[0] = bucket(me)
-    a2a(tiles - 1).start()
-
+    for step in order:
+        rcv[step, sent:] = jnp.zeros((members + META - sent, slots), BF16)
+    pl.semaphore_wait(barrier, tiles - 1 + lags - 1)
+    for step in order:
+        a2a(step).start()
+
+    ens_load = pltpu.make_async_copy(ens_hbm, ens, move_sem.at[0])
+    ens_load.start()
+    arrivals = [0] + list(order)
     for first in range(0, tiles, group):
-        for step in range(max(first, 1), first + group):
+        for step in arrivals[max(first, 1) : first + group]:
             a2a(step).wait_recv()
-        obs = jnp.concatenate([rcv[step] for step in range(first, first + group)], axis=1)
+        obs = jnp.concatenate([rcv[step] for step in arrivals[first : first + group]], axis=1)
         pert = obs[0:members].astype(F32)
         info = obs[members:].astype(F32)
         obs_weight = info[0:1]
         places = info[2:3] * BASE + info[3:4]
-        for k in range(points + 2 * half):
-            center = float((k - half) * SPACING + SPACING // 2)
-            taper = jnp.maximum(1.0 - jnp.abs(places - center) / radius, 0.0)
-            rho = taper * taper * obs_weight
-            scaled = (pert * rho).astype(BF16)
-            part = lax.dot_general(scaled, obs, NT, preferred_element_type=F32)
-            if first == 0:
-                acc[k] = part
-            else:
-                acc[k] += part
+
+        def moments(ks, obs=obs, pert=pert, places=places, obs_weight=obs_weight, first=first):
+            for k in ks:
+                center = float((k - half) * SPACING + SPACING // 2)
+                taper = jnp.maximum(1.0 - jnp.abs(places - center) / radius, 0.0)
+                rho = taper * taper * obs_weight
+                scaled = (pert * rho).astype(BF16)
+                part = lax.dot_general(scaled, obs, NT, preferred_element_type=F32)
+                if first == 0:
+                    acc[k] = part
+                else:
+                    acc[k] += part
+
+        if first + group < tiles:
+            moments(range(points + 2 * half))
 
     lane = lax.broadcasted_iota(jnp.int32, (members, pair), 1)
     low = lane < members
@@ -135,34 +162,6 @@
 
     def drive_of(a):
         return acc[a, :, members + 1 : members + 2]
-
-    pairs_side = (half + 2) // 2
-    last = points + 2 * half - 1
-    left_own = jnp.concatenate([jnp.zeros((members, members), F32), acc[0, :, 0:members]], axis=1)
-    for j in range(half + 1):
-        left_own = jnp.where(lane == j, drive_of(j), left_own)
-    to_left[0] = left_own
-    for i in range(1, pairs_side):
-        to_left[i] = joined(2 * i - 1, 2 * i)
-    right_own = jnp.concatenate([acc[last, :, 0:members], jnp.zeros((members, members), F32)], axis=1)
-    for j in range(half + 1):
-        right_own = jnp.where(lane == members + j, drive_of(last - half + j), right_own)
-    to_right[pairs_side - 1] = right_own
-    for i in range(pairs_side - 1):
-        to_right[i] = joined(last - half + 2 * i, last - half + 2 * i + 1)
-
-    eye = jnp.where(
-        lax.rem(lane, members) == lax.broadcasted_iota(jnp.int32, (members, pair), 0), 1.0, 0.0
-    )
-    mask_low = jnp.where(low, 1.0, 0.0).astype(BF16)
-    mask_high = jnp.where(low, 0.0, 1.0).astype(BF16)
-
-    def diagonal(x):
-        return jnp.concatenate([x * mask_low, x * mask_high], axis=0)
-
-    def blocks(x):
-        hi, lo = halves(x)
-        return stationary(diagonal(hi), diagonal(lo))
 
     left_copy = pltpu.make_async_remote_copy(
         src_ref=to_left, dst_ref=from_right, send_sem=halo_send.at[0], recv_sem=halo_recv.at[0],
@@ -172,8 +171,42 @@
         src_ref=to_right, dst_ref=from_left, send_sem=halo_send.at[1], recv_sem=halo_recv.at[1],
         device_id={"space": lax.rem(me + 1, tiles)},
     )
+
+    pairs_side = (half + 2) // 2
+    last = points + 2 * half - 1
+    moments(range(half + 1))
+    left_own = jnp.concatenate([jnp.zeros((members, members), F32), acc[0, :, 0:members]], axis=1)
+    for j in range(half + 1):
+        left_own = jnp.where(lane == j, drive_of(j), left_own)
+    to_left[0] = left_own
+    for i in range(1, pairs_side):
+        to_left[i] = joined(2 * i - 1, 2 * i)
+    moments(range(last - half, last + 1))
     left_copy.start()
+    right_own = jnp.concatenate([acc[last, :, 0:members], jnp.zeros((members, members), F32)], axis=1)
+    for j in range(half + 1):
+        right_own = jnp.where(lane == members + j, drive_of(last - half + j), right_own)
+    to_right[pairs_side - 1] = right_own
+    for i in range(pairs_side - 1):
+        to_right[i] = joined(last - half + 2 * i, last - half + 2 * i + 1)
+
+    moments(range(half + 1, half + 3))
     right_copy.start()
+    moments(range(half + 3, last - half))
+
+    eye = jnp.where(
+        lax.rem(lane, members) == lax.broadcasted_iota(jnp.int32, (members, pair), 0), 1.0, 0.0
+    )
+    mask_low = jnp.where(low, 1.0, 0.0).astype(BF16)
+    mask_high = jnp.where(low, 0.0, 1.0).astype(BF16)
+
+    def diagonal(x):
+        return jnp.concatenate([x * mask_low, x * mask_high], axis=0)
+
+    def blocks(x):
+        hi, lo = halves(x)
+        return stationary(diagonal(hi), diagonal(lo))
+
 
     count = (points + 2) // 2
     own_pairs = [joined(half - 1 + 2 * i, half + 2 * i) for i in range(count)]
@@ -257,8 +290,30 @@
         for i in range(count):
             longer = times(results[i], blocks(theirs[step - 1, i]))
             results[i] = jnp.where(later, longer, results[i])
-    for i in range(count):
-        out_ref[i] = results[i].astype(BF16)
+    turned = jnp.concatenate([results[i].T.astype(BF16) for i in range(count)], axis=0)
+    ens_load.wait()
+    stores = []
+    half_span = SPACING // 2
+    for s in range(points + 1):
+        start = max(s * SPACING - half_span, 0)
+        stop = min(s * SPACING + half_span, columns)
+        both = jnp.dot(
+            turned[s * members : (s + 2) * members], ens[:, start:stop],
+            preferred_element_type=F32,
+        )
+        along = lax.broadcasted_iota(jnp.int32, (1, stop - start), 1).astype(F32)
+        second = (along + float(start - (s * SPACING - half_span))) / SPACING
+        mixed = both[0:members] * (1.0 - second) + both[members:] * second
+        out[:, start:stop] = mixed.astype(BF16)
+        if s % 3 == 2:
+            first = max((s - 2) * SPACING - half_span, 0)
+            store = pltpu.make_async_copy(
+                out.at[:, first:stop], out_hbm.at[:, first:stop], move_sem.at[1 + s // 3]
+            )
+            store.start()
+            stores.append(store)
+    for store in stores:
+        store.wait()
 
     for step in range(1, tiles):
         a2a(step).wait_send()
@@ -266,25 +321,6 @@
     right_copy.wait_send()
     for step in range(1, lags):
         lag_copy(step).wait_send()
-
-
-def apply_kernel(members, columns, weights_ref, ens_ref, out_ref):
-    points = columns // SPACING
-    turned = jnp.concatenate(
-        [weights_ref[i].astype(F32).T.astype(BF16) for i in range((points + 2) // 2)], axis=0
-    )
-    half_span = SPACING // 2
-    for s in range(points + 1):
-        start = max(s * SPACING - half_span, 0)
-        stop = min(s * SPACING + half_span, columns)
-        both = jnp.dot(
-            turned[s * members : (s + 2) * members], ens_ref[:, start:stop],
-            preferred_element_type=F32,
-        )
-        along = lax.broadcasted_iota(jnp.int32, (1, stop - start), 1).astype(F32)
-        second = (along + float(start - (s * SPACING - half_span))) / SPACING
-        mixed = both[0:members] * (1.0 - second) + both[members:] * second
-        out_ref[:, start:stop] = mixed.astype(BF16)
 
 
 def per_device(ensemble, obs_pert, obs_innov, obs_rinv, obs_tile, obs_column, obs_count):
@@ -300,13 +336,21 @@
     pair = 2 * members
     rows = members + META
     side = ((half + 2) // 2, members, pair)
-    vmem = pl.BlockSpec(memory_space=pltpu.VMEM)
     products = pl.pallas_call(
         functools.partial(weights_kernel, tiles, lags, slots, group, columns),
-        out_shape=jax.ShapeDtypeStruct((count, members, pair), BF16),
-        in_specs=[vmem] * 5 + [pl.BlockSpec(memory_space=pltpu.SMEM)],
-        out_specs=vmem,
+        out_shape=jax.ShapeDtypeStruct((members, columns), BF16),
+        in_specs=[pl.BlockSpec(memory_space=pltpu.HBM)] * 7,
+        out_specs=pl.BlockSpec(memory_space=pltpu.HBM),
         scratch_shapes=[
+            pltpu.VMEM((members, columns), BF16),
+            pltpu.VMEM((members, columns), BF16),
+            pltpu.SemaphoreType.DMA((1 + (points + 1) // 3,)),
+            pltpu.VMEM((1, own), BF16),
+            pltpu.VMEM((1, own), BF16),
+            pltpu.VMEM((1, own), jnp.int32),
+            pltpu.VMEM((1, own), jnp.int32),
+            pltpu.SMEM((1, 1), jnp.int32),
+            pltpu.SemaphoreType.DMA((6,)),
             pltpu.VMEM((rows, own), BF16),
             pltpu.VMEM((tiles, rows, slots), BF16),
             pltpu.VMEM((tiles, rows, slots), BF16),
@@ -326,15 +370,8 @@
         ],
         compiler_params=pltpu.CompilerParams(collective_id=0, has_side_effects=True),
         name="ensemble_weights",
-    )(obs_pert[0], obs_innov, obs_rinv, obs_tile[:, :, 0], obs_column, obs_count)
-    analysis = pl.pallas_call(
-        functools.partial(apply_kernel, members, columns),
-        out_shape=jax.ShapeDtypeStruct((members, columns), BF16),
-        in_specs=[vmem] * 2,
-        out_specs=vmem,
-        name="apply_weights",
-    )(products, ensemble[0])
-    return analysis[None]
+    )(obs_pert[0], obs_innov, obs_rinv, obs_tile[:, :, 0], obs_column, obs_count, ensemble[0])
+    return products[None]
 
 
 def solution(mesh):

time: 32.3 us -> 28.5 us (0.88)
  Pallas kernels: 31.4 us -> 25.8 us
  local copies, waits for them, and re-layouts: 0 us -> 1.87 us
    pallas_call x1, Pallas kernels: 29.1 us -> 25.8 us  [per_device(): pl.pallas_call(functools.partial(weights_kernel, tiles, lags, slots, grou...]
    pallas_call x1 -> x0, Pallas kernels: 2.38 us -> none  [per_device(): pl.pallas_call(functools.partial(apply_kernel, members, columns), out_sha...]
    unnamed x0 -> x1, local copies, waits for them, and re-layouts: none -> 1.87 us
where the time goes in v2:
time: 28.5 us; the launch traced here: 28.3 us
  Pallas kernels  25.8 us (91%)
  local copies, waits for them, and re-layouts  1.87 us (7%)
  between operations  0.66 us (2%)
    pallas_call x1, Pallas kernels, per_device(): pl.pallas_call(functools.partial(weights_kernel, tiles, lags, slots, grou...  25.8 us
    unnamed x1, local copies, waits for them, and re-layouts  1.87 us

profile of v2, /device:TPU:1, one launch (start us, length us, event | category | flops | bytes accessed | tf_op | source)
XLA Modules:
  0.0 28.3 jit_solution(9435876501087664637)
XLA Ops:
  0.7 25.8 %ensemble_weights.1 = bf16[64,4096]{1,0:T(8,128)(2,1)} custom-call(bf16[64,1024]{1,0:T(8,128)(2,1)} %bitcast.6, bf16[1,1024]{1,0:T(2,128)(2,1)} %innov_hbm.1, bf16[1,1024]{1,0:T(2,128)(2,1)} %rinv_hbm.1, s32[1,1024]{1,0:T(1,128)} %bitcast.7, s32[1,1024]{1,0:T(1,128)} %col_hbm.1, s32[1,1]{1,0:T(1,128)S(6)} %copy.9.count_hbm, bf16[64,4096]{1,0:T(8,128)(2,1)} %bitcast.5), custom_call_target="tpu_custom_call" | custom-call | tf_op jit(solution)/shard_map/ensemble_weights/pallas_call | solution.py:339
  26.5 1.9 %copy.10 = bf16[1,64,4096]{2,1,0:T(8,128)(2,1)} copy(bf16[1,64,4096]{2,1,0:T(8,128)(2,1)} %bitcast.4) | data formatting | bytes 1048576
